TPU v7x, 256 devices: a whole 4x4x8 slice. The times are simulated.
256 devices in a mesh: row: 16 (over z_lo, y), col: 16 (over z_hi, x, core).
Axes of the slice: x: 4, y: 4, z: 8 (z_hi: 2, z_lo: 4; z = z_hi * 4 + z_lo), core: 2. Of those that a mesh axis runs over, the one named last changes fastest.
Arguments:
- orbitals: float32 [2048, 28672], P(('row', 'col')), may hold values from -0.03125 to 0.03125
- applied: float32 [2048, 28672], P(('row', 'col')), may hold values from -24 to 24
Outputs:
- hamiltonian: float32 [2048, 2048], P('col', 'row')
- intersection: float32 [2048, 2048], P('col', 'row')
All inputs are finite; a program needn't handle non-finite values.
Results may differ from a plain program's by a relative error of at most 0.000098.
Values sent between devices are 32-bit elements; how exact they have to be, the bound alone decides.
A program may use at most 64 MiB of HBM per device.

v0:
```python
import jax
import jax.numpy as jnp
from jax import lax
from jax.sharding import PartitionSpec as P


def sent_together(arrays, axis, dim, along):
    both = jnp.concatenate(arrays, axis=along)
    result, at, done = (lax.psum_scatter(both, axis, scatter_dimension=dim, tiled=True), 0, [])
    for a in arrays:
        done.append(lax.slice_in_dim(result, at, at + a.shape[along], axis=along))
        at += a.shape[along]
    return tuple(done)


def product(left, right):
    return lax.dot_general(
        left,
        right,
        (((1,), (1,)), ((), ())),
        precision=lax.Precision.HIGHEST,
        preferred_element_type=jnp.float32,
    )


def shards(orbitals, applied):
    mine_orb, mine_app = (
        lax.all_to_all(orbitals, "col", split_axis=1, concat_axis=0, tiled=True),
        lax.all_to_all(applied, "col", split_axis=1, concat_axis=0, tiled=True),
    )
    every_orb = lax.all_gather(mine_orb, "row", axis=0, tiled=True)
    ham_part = product(every_orb, mine_app)
    ovl_part = product(every_orb, mine_orb)
    hamiltonian, intersection = sent_together((ham_part, ovl_part), "col", 0, 1)
    return (hamiltonian, intersection)


def solution(mesh):
    placed = (P(("row", "col"), None), P(("row", "col"), None))
    return jax.shard_map(
        shards,
        mesh=mesh,
        in_specs=placed,
        out_specs=(P("col", "row"), P("col", "row")),
        check_vma=False,
    )
```

profile of v0, /device:TPU:6, one launch (start us, length us, event | category | flops | bytes accessed | tf_op | source)
XLA Modules:
  0.0 355.2 jit_solution(10867969578513426620)
XLA Ops:
  7.2 0.0 all-gather.2.cloned.1.call-start
  7.2 30.7 %all_to_all.38 = f32[8,16,1792]{2,0,1:T(8,128)} all-to-all(f32[8,16,1792]{2,0,1:T(8,128)} %bitcast.15), channel_id=1, replica_groups=mesh['row'=16,'col'=16] {'col'}, dimensions={1} | all-to-all | bytes 1835008 | tf_op jit(solution)/shard_map/all_to_all | solution.py:28
  37.9 0.0 all-gather.2.cloned.1.call-update
  37.9 5.7 %all-to-all-start.1 = ((f32[8,16,1792]{2,0,1:T(8,128)}), f32[8,16,1792]{2,0,1:T(8,128)S(1)}, u32[]{:S(2)}, u32[]{:S(2)}) async-start(f32[8,16,1792]{2,0,1:T(8,128)} %bitcast.16), calls=%async_computation.1 | async-start | bytes 1835008 | tf_op jit(solution)/shard_map/all_to_all | solution.py:29
  43.6 0.0 reduce-scatter.2.cloned.1.call-start
  43.7 178.5 %all-gather.2.cloned.1.call-done = f32[2048,1792]{1,0:T(8,128)} async-done(((f32[128,1792]{1,0:T(8,128)}), f32[2048,1792]{1,0:T(8,128)}) %all-gather.2.cloned.1.call-update) | async-done | bytes 14680080 | tf_op jit(solution)/shard_map/all_gather | solution.py:31
  222.1 18.5 %fusion.2 = f32[2048,128]{0,1:T(8,128)S(1)} fusion(f32[2048,1792]{1,0:T(8,128)} %all-gather.2.cloned.1.call-done, f32[8,16,1792]{2,0,1:T(8,128)} %all_to_all.38), kind=kOutput, calls=%fused_computation.3 | convolution fusion | flops 5637144576 | bytes 16646144 | tf_op jit(solution)/shard_map/dot_general | solution.py:17
  240.7 0.0 all-to-all-done.1
  240.7 18.3 %fusion = f32[2048,128]{0,1:T(8,128)S(1)} fusion(f32[2048,1792]{1,0:T(8,128)} %all-gather.2.cloned.1.call-done, f32[8,16,1792]{2,0,1:T(8,128)S(1)} %all-to-all-done.1), kind=kOutput, calls=%fused_computation.1 | convolution fusion | flops 5637144576 | bytes 16646144 | tf_op jit(solution)/shard_map/dot_general | solution.py:17
  259.0 1.5 pad_maximum_fusion
  260.5 0.0 reduce-scatter.2.cloned.1.call-update
  260.5 85.5 %reduce-scatter.2.cloned.1.call-done = f32[128,256]{0,1:T(8,128)} async-done(((f32[2048,256]{0,1:T(8,128)}), f32[128,256]{0,1:T(8,128)}) %reduce-scatter.2.cloned.1.call-update) | async-done | bytes 131088 | tf_op jit(solution)/shard_map/reduce_scatter | solution.py:9
  346.0 0.9 fusion.4
  346.9 0.7 copy.5
  347.6 0.7 copy.4
Async XLA Ops:
  7.2 215.0 %all-gather.2.cloned.1.call-start = ((), (), s32[]{:S(2)}) async-start(), calls=%async_computation.3 | async-start | bytes 15597568 | tf_op jit(solution)/shard_map/all_gather | solution.py:31
  37.9 202.8 %all-to-all-start.1 = ((f32[8,16,1792]{2,0,1:T(8,128)}), f32[8,16,1792]{2,0,1:T(8,128)S(1)}, u32[]{:S(2)}, u32[]{:S(2)}) async-start(f32[8,16,1792]{2,0,1:T(8,128)} %bitcast.16), calls=%async_computation.1 | async-start | bytes 1835008 | tf_op jit(solution)/shard_map/all_to_all | solution.py:29
  43.6 302.4 %reduce-scatter.2.cloned.1.call-start = ((), (), s32[]{:S(2)}) async-start(), calls=%async_computation.4 | async-start | bytes 2228224 | tf_op jit(solution)/shard_map/reduce_scatter | solution.py:9
Sparse Core Ops, SparseCore 0:
  38.0 184.0 all-gather.1
  260.7 85.2 reduce-scatter.1
where the time goes:
time: 356 us; the launch traced here: 355 us
  waiting for transfers between devices  264 us (74%)
  matrix products  36.9 us (10%)
  blocking collectives  30.7 us (9%)
  between operations  14.1 us (4%)
  starting transfers between devices  5.8 us (2%)
    all_gather x1, waiting for transfers between devices, shards(): every_orb = lax.all_gather(mine_orb, 'row', axis=0, tiled=True)  178 us
    reduce_scatter x1, waiting for transfers between devices, sent_together(): lax.psum_scatter(both, axis, scatter_dimension=dim, tiled=True)  85.5 us
    dot_general x2, matrix products, product(): lax.dot_general(left, right, (((1,), (1,)), ((), ())), precision=lax.Prec...  36.9 us
    all_to_all x1, blocking collectives, shards(): lax.all_to_all(orbitals, 'col', split_axis=1, concat_axis=0, tiled=True)  30.7 us
  transfers between devices with their start and end apart: 3, of which 2 were waited for; matrix products, arithmetic and copies ran while one was open for 5% of the time, Pallas kernels for 0%

commit v1 on v0

v1 whole, which is shorter than its diff:
```python
import jax
import jax.numpy as jnp
from jax import lax
from jax.sharding import Mesh, PartitionSpec as P

PLANE = ("zl", "zh", "x", "core")


def halves(a):
    hi = lax.reduce_precision(a, 8, 7)
    lo = a - hi
    return hi.astype(jnp.bfloat16), lo.astype(jnp.bfloat16)


def product(left, right):
    def dot(a, b):
        return lax.dot_general(
            a, b, (((1,), (1,)), ((), ())), preferred_element_type=jnp.float32
        )

    (lh, ll), (rh, rl) = halves(left), halves(right)
    return dot(lh, rh) + (dot(lh, rl) + dot(ll, rh))


def shards(orbitals, applied):
    orb = lax.all_to_all(orbitals, PLANE, split_axis=1, concat_axis=0, tiled=True)
    app = lax.all_to_all(applied, PLANE, split_axis=1, concat_axis=0, tiled=True)
    every = lax.all_gather(orb, "y", axis=0, tiled=False)
    k = orb.shape[1]
    every = every.reshape(4, 4, 128, k).transpose(1, 0, 2, 3).reshape(2048, k)
    parts = product(every, jnp.concatenate([orb, app], axis=0))
    parts = parts.reshape(16, 128, 2, 4, 128).transpose(3, 0, 2, 1, 4)
    parts = parts.reshape(64, 2, 128, 128)
    mine = lax.psum_scatter(parts, PLANE, scatter_dimension=0, tiled=True)
    return mine[0, 1], mine[0, 0]


def solution(mesh):
    fine = Mesh(mesh.devices.reshape(4, 4, 2, 4, 2), ("zl", "y", "zh", "x", "core"))
    placed = (P(("zl", "y", "zh", "x", "core"), None),) * 2
    out = P(("zh", "x", "core"), ("zl", "y"))
    return jax.shard_map(
        shards, mesh=fine, in_specs=placed, out_specs=(out, out), check_vma=False
    )
```

time: 356 us -> 516 us (1.45); the launches traced: 355 us -> 507 us
  waiting for transfers between devices: 264 us -> 392 us
  local copies, waits for them, and re-layouts: 2.34 us -> 42.4 us
  matrix products: 36.9 us -> 12.5 us
  blocking collectives: 30.7 us -> 38.6 us
    reduce_scatter x1, waiting for transfers between devices: 85.5 us -> 357 us  [shards(): mine = lax.psum_scatter(parts, PLANE, scatter_dimension=0, tiled=True)]
    all_gather x1, waiting for transfers between devices: 178 us -> 35.1 us  [shards(): every = lax.all_gather(orb, 'y', axis=0, tiled=False)]
    dot_general x2 -> x3, matrix products: 36.9 us -> 12.5 us  [dot(): lax.dot_general(a, b, (((1,), (1,)), ((), ())), preferred_element_type=jn...]
    reshape x0 -> x3, local copies, waits for them, and re-layouts: none -> 16.5 us  [shards(): every = every.reshape(4, 4, 128, k).transpose(1, 0, 2, 3).reshape(2048, k)]
    transpose x0 -> x1, local copies, waits for them, and re-layouts: none -> 10.1 us  [shards(): parts = parts.reshape(16, 128, 2, 4, 128).transpose(3, 0, 2, 1, 4)]
    all_to_all x1, blocking collectives: 30.7 us -> 38.6 us  [shards(): lax.all_to_all(orbitals, PLANE, split_axis=1, concat_axis=0, tiled=True)]
    unnamed x2 -> x5, local copies, waits for them, and re-layouts: 1.46 us -> 8.62 us
  transfers between devices with their start and end apart: 3 -> 3, of which waited for: 2 -> 2; matrix products, arithmetic and copies ran while one was open for 5% -> 4% of each run, Pallas kernels for 0% -> 0%
where the time goes in v1:
time: 516 us; the launch traced here: 507 us
  waiting for transfers between devices  392 us (76%)
  local copies, waits for them, and re-layouts  42.4 us (8%)
  blocking collectives  38.6 us (7%)
  between operations  14.1 us (3%)
  matrix products  12.5 us (2%)
  starting transfers between devices  7.77 us (2%)
    reduce_scatter x1, waiting for transfers between devices, shards(): mine = lax.psum_scatter(parts, PLANE, scatter_dimension=0, tiled=True)  357 us
    all_to_all x1, blocking collectives, shards(): lax.all_to_all(orbitals, PLANE, split_axis=1, concat_axis=0, tiled=True)  38.6 us
    all_gather x1, waiting for transfers between devices, shards(): every = lax.all_gather(orb, 'y', axis=0, tiled=False)  35.1 us
    reshape x3, local copies, waits for them, and re-layouts, shards(): every = every.reshape(4, 4, 128, k).transpose(1, 0, 2, 3).reshape(2048, k)  16.5 us
    dot_general x3, matrix products, dot(): lax.dot_general(a, b, (((1,), (1,)), ((), ())), preferred_element_type=jn...  12.5 us
  transfers between devices with their start and end apart: 3, of which 2 were waited for; matrix products, arithmetic and copies ran while one was open for 4% of the time, Pallas kernels for 0%

profile of v1, /device:TPU:6, one launch (start us, length us, event | category | flops | bytes accessed | tf_op | source)
XLA Modules:
  0.0 507.3 jit_solution(13280766706222515554)
XLA Ops:
  7.2 0.0 all-gather.2.cloned.1.call-start
  7.2 1.7 all_to_all.28
  8.9 0.0 copy-start.1
  8.9 0.6 copy.11
  9.5 38.6 %all_to_all.38 = f32[8,64,448]{2,0,1:T(8,128)S(1)} all-to-all(f32[8,64,448]{2,0,1:T(8,128)S(1)} %copy.11), channel_id=1, replica_groups=mesh['zl'=4,'y'=4,'zh'=2,'x'=4,'core'=2] {'zl','zh','x','core'}, dimensions={1} | all-to-all | bytes 1835008 | tf_op jit(solution)/shard_map/all_to_all | solution.py:26
  48.1 1.3 copy.13
  49.4 0.0 all-gather.2.cloned.1.call-update
  49.4 0.0 copy-done.1
  49.4 0.5 all_to_all.32
  49.9 1.6 copy.12
  51.5 7.5 %all-to-all-start.1 = ((f32[8,64,448]{2,0,1:T(8,128)}), f32[8,64,448]{2,0,1:T(8,128)S(1)}, u32[]{:S(2)}, u32[]{:S(2)}) async-start(f32[8,64,448]{2,0,1:T(8,128)} %copy.12), calls=%async_computation.1 | async-start | bytes 2097152 | tf_op jit(solution)/shard_map/all_to_all | solution.py:27
  59.1 0.2 reduce-scatter.2.cloned.1.call-start
  59.3 35.1 %all-gather.2.cloned.1.call-done = f32[4,512,448]{1,2,0:T(8,128)} async-done(((f32[1,512,448]{1,2,0:T(8,128)}), f32[4,512,448]{1,2,0:T(8,128)}) %all-gather.2.cloned.1.call-update) | async-done | bytes 3670032 | tf_op jit(solution)/shard_map/all_gather | solution.py:28
  94.4 5.1 %reshape.23 = f32[4,4,128,448]{2,1,3,0:T(4,128)} reshape(f32[4,512,448]{1,2,0:T(8,128)} %all-gather.2.cloned.1.call-done) | data formatting | bytes 7340032 | tf_op jit(solution)/shard_map/reshape | solution.py:30
  99.5 6.2 %copy.20 = f32[4,4,128,448]{2,0,1,3:T(4,128)} copy(f32[4,4,128,448]{2,1,3,0:T(4,128)} %reshape.23) | data formatting | bytes 7340032 | tf_op jit(solution)/shard_map/reshape | solution.py:30
  105.7 5.3 %reshape.24 = f32[2048,448]{0,1:T(8,128)} reshape(f32[4,4,128,448]{2,1,0,3:T(4,128)} %bitcast.45) | data formatting | bytes 7340032 | tf_op jit(solution)/shard_map/reshape | solution.py:30
  111.0 0.0 all-to-all-done.1
  111.0 0.0 copy-start
  111.0 4.5 fusion.4
  115.5 0.0 copy-done
  115.5 2.3 fusion.7
  117.9 5.6 %fusion.1 = f32[128,8,16,128]{3,1,2,0:T(8,128)} fusion(f32[2048,1024]{0,1:T(8,128)S(1)} %fusion.4, f32[1024,2048]{1,0:T(8,128)S(1)} %fusion.7, f32[512,448]{1,0:T(8,128)S(1)} %bitcast.44, f32[512,448]{1,0:T(8,128)S(1)} %bitcast.41, f32[2048,448]{0,1:T(8,128)S(1)} %copy-done), kind=kOutput, calls=%fused_computation.2 | convolution fusion | flops 1886912512 | bytes 30670848 | tf_op jit(solution)/shard_map/dot_general | solution.py:17
  123.5 8.6 %copy.18 = f32[128,8,16,128]{3,2,1,0:T(8,128)} copy(f32[128,8,16,128]{3,1,2,0:T(8,128)} %fusion.1) | data formatting | bytes 16777216
  132.1 10.1 %copy.16 = f32[4,16,2,128,128]{4,3,2,1,0:T(8,128)} copy(f32[4,16,2,128,128]{3,1,4,0,2:T(8,128)} %bitcast.37) | data formatting | bytes 16777216 | tf_op jit(solution)/shard_map/transpose | solution.py:32
  142.2 0.0 reduce-scatter.2.cloned.1.call-update
  142.2 356.7 %reduce-scatter.2.cloned.1.call-done = f32[1,2,128,128]{3,2,1,0:T(8,128)} async-done(((f32[64,2,128,128]{3,2,1,0:T(8,128)}), f32[1,2,128,128]{3,2,1,0:T(8,128)}) %reduce-scatter.2.cloned.1.call-update) | async-done | bytes 131088 | tf_op jit(solution)/shard_map/reduce_scatter | solution.py:34
  498.9 1.5 slice_bitcast_fusion
Async XLA Ops:
  7.2 87.3 %all-gather.2.cloned.1.call-start = ((), (), s32[]{:S(2)}) async-start(), calls=%async_computation.3 | async-start | bytes 4587520 | tf_op jit(solution)/shard_map/all_gather | solution.py:28
  8.9 40.5 %copy-start.1 = (f32[8,28672]{1,0:T(8,128)S(1)}, f32[8,28672]{1,0:T(8,128)}, u32[]{:S(2)}) copy-start(f32[8,28672]{1,0:T(8,128)} %param.3) | copy-start | bytes 2752516
  51.5 59.4 %all-to-all-start.1 = ((f32[8,64,448]{2,0,1:T(8,128)}), f32[8,64,448]{2,0,1:T(8,128)S(1)}, u32[]{:S(2)}, u32[]{:S(2)}) async-start(f32[8,64,448]{2,0,1:T(8,128)} %copy.12), calls=%async_computation.1 | async-start | bytes 2097152 | tf_op jit(solution)/shard_map/all_to_all | solution.py:27
  59.1 439.8 %reduce-scatter.2.cloned.1.call-start = ((), (), s32[]{:S(2)}) async-start(), calls=%async_computation.4 | async-start | bytes 8519680 | tf_op jit(solution)/shard_map/reduce_scatter | solution.py:34
  111.0 4.6 copy-start
Sparse Core Ops, SparseCore 0:
  49.5 44.8 all-gather.1
  142.4 356.4 reduce-scatter.1

commit v2 on v1

v2 whole, which is shorter than its diff:
```python
import jax
import jax.numpy as jnp
from jax import lax
from jax.experimental import pallas as pl
from jax.experimental.pallas import tpu as pltpu
from jax.sharding import PartitionSpec as P

MESH = pl.DeviceIdType.MESH
DEPTH = 896
div, rem = lax.div, lax.rem


def drain(ref, sem):
    pltpu.make_async_copy(ref, ref, sem).wait()


def offset_at(t):
    odd = rem(t, 2)
    return odd * div(t + 1, 2) + (1 - odd) * rem(8 - div(t, 2), 8)


def split3(value, low_at):
    hi = value.astype(jnp.bfloat16)
    lo = (value - hi.astype(jnp.float32)).astype(jnp.bfloat16)
    return [lo if n == low_at else hi for n in range(3)]


def kernel(
    orb_hbm, app_hbm, ham_ref, ovl_ref,
    inp, orb, app, left, right, part, xbuf, red, zbuf,
    in_sem, loc_sem, a_send, a_recv, y_send, y_recv, d_send, d_recv,
    x_send, x_recv, z_send, z_recv,
):
    row, col = lax.axis_index("row"), lax.axis_index("col")
    zl, y = div(row, 4), rem(row, 4)
    zh, x, s = div(col, 8), rem(div(col, 2), 4), rem(col, 2)
    z = zh * 4 + zl
    giver = rem(y, 2)
    role_a = s == giver
    role_b = s != giver
    own = div(y, 2)

    def device(zz, yy, xx, ss):
        return (rem(zz, 4) * 4 + yy, div(zz, 4) * 8 + xx * 2 + ss)

    def send(src, dst, send_sem, recv_sem, target):
        pltpu.make_async_remote_copy(
            src_ref=src, dst_ref=dst, send_sem=send_sem, recv_sem=recv_sem,
            device_id=target, device_id_type=MESH,
        ).start()

    sibling = device(z, y, x, 1 - s)
    y_up, y_down = device(z, rem(y + 1, 4), x, s), device(z, rem(y + 3, 4), x, s)
    xr, xl, x2 = rem(x + 1, 4), rem(x + 3, 4), rem(x + 2, 4)

    loads = [
        pltpu.make_async_copy(orb_hbm, inp.at[0], in_sem.at[0]),
        pltpu.make_async_copy(app_hbm, inp.at[1], in_sem.at[1]),
    ]
    for load in loads:
        load.start()

    barrier = pltpu.get_barrier_semaphore()

    def greet(n, carry):
        p = rem(z * 8 + x * 2 + s + n, 64)
        pl.semaphore_signal(
            barrier, inc=1, device_id=device(div(p, 8), y, div(rem(p, 8), 2), rem(p, 2)),
            device_id_type=MESH,
        )
        return carry

    lax.fori_loop(1, 64, greet, 0)
    for target in (y_up, y_down):
        pl.semaphore_signal(barrier, inc=1, device_id=target, device_id_type=MESH)
    for load in loads:
        load.wait()
    pl.semaphore_wait(barrier, 65)

    slot = pl.ds(pl.multiple_of(zl * 128 + col * 8, 8), 8)
    orb_slot, app_slot = orb.at[own, slot], app.at[slot]

    def columns(zz, xx):
        return pl.ds(pl.multiple_of((zz * 4 + xx) * DEPTH, 128), DEPTH)

    def scatter(which, dst, core):
        def step(n, carry):
            d = offset_at(div(n, 4))
            zz, xx = rem(z + d, 8), rem(x + rem(n, 4), 4)
            send(
                inp.at[which, :, columns(zz, xx)], dst, a_send,
                a_recv.at[rem(8 - d, 8)], device(zz, y, xx, core),
            )
            return carry

        lax.fori_loop(1, 32, step, 0)

    orb_mine, app_mine = inp.at[0, :, columns(z, x)], inp.at[1, :, columns(z, x)]

    @pl.when(role_a)
    def _():
        pltpu.make_async_copy(orb_mine, orb_slot, loc_sem).start()

    @pl.when(role_b)
    def _():
        send(orb_mine, orb_slot, a_send, a_recv.at[0], sibling)

    scatter(0, orb_slot, giver)

    @pl.when(role_a)
    def _():
        send(app_mine, app_slot, a_send, a_recv.at[0], sibling)

    @pl.when(role_b)
    def _():
        pltpu.make_async_copy(app_mine, app_slot, loc_sem).start()

    scatter(1, app_slot, 1 - giver)

    def rows_of(t):
        g = offset_at(t)
        zz = rem(z + g, 8)
        return g, pl.multiple_of(rem(zz, 4) * 128 + div(zz, 4) * 64, 64)

    def arrived(t, g):
        @pl.when(t == 0)
        def _():
            drain(app.at[pl.ds(0, 56)], a_recv.at[0])
            drain(app.at[pl.ds(0, 8)], loc_sem)

        @pl.when(t > 0)
        def _():
            drain(app.at[pl.ds(0, 64)], a_recv.at[g])

    @pl.when(role_a)
    def _():
        def pass_on(t, carry):
            g, first = rows_of(t)
            arrived(t, g)
            block = orb.at[own, pl.ds(first, 64)]
            send(block, block, y_send, y_recv.at[0, g], y_up)
            send(block, block, y_send, y_recv.at[1, g], y_down)
            send(block, orb.at[2, pl.ds(first, 64)], d_send, d_recv, sibling)
            return carry

        lax.fori_loop(0, 8, pass_on, 0)

        def take(t, carry):
            for way in range(2):
                drain(app.at[pl.ds(0, 32)], y_recv.at[way, t])
            return carry

        lax.fori_loop(0, 8, take, 0)

    @pl.when(role_b)
    def _():
        below, above = div(rem(y + 3, 4), 2), div(rem(y + 1, 4), 2)

        def pass_on(t, carry):
            g, first = rows_of(t)
            drain(app.at[pl.ds(0, 64)], y_recv.at[0, g])
            low = orb.at[below, pl.ds(first, 32)]
            send(low, low, y_send, y_recv.at[0, g], y_up)
            drain(app.at[pl.ds(0, 64)], y_recv.at[1, g])
            high = orb.at[above, pl.ds(first + 32, 32)]
            send(high, high, y_send, y_recv.at[1, g], y_down)
            return carry

        lax.fori_loop(0, 8, pass_on, 0)
        drain(app, d_recv)

    def set_left(n, carry):
        at = pl.ds(pl.multiple_of(rem(n, 8) * 64, 64), 64)
        for k, piece in enumerate(split3(orb[div(n, 8), at, :], 1)):
            left[div(n, 8), at, k * DEPTH : (k + 1) * DEPTH] = piece
        return carry

    def set_right(read):
        def step(n, carry):
            at = pl.ds(pl.multiple_of(n * 64, 64), 64)
            for k, piece in enumerate(split3(read(at), 2)):
                right[at, k * DEPTH : (k + 1) * DEPTH] = piece
            return carry

        lax.fori_loop(0, 8, step, 0)

    def multiply(mat):
        def step(n, carry):
            plane, tile = div(n, 2), pl.multiple_of(rem(n, 2) * 256, 256)
            part[mat, plane, :, pl.ds(tile, 256)] = lax.dot_general(
                left[plane], right[pl.ds(tile, 256), :],
                (((1,), (1,)), ((), ())), preferred_element_type=jnp.float32,
            )
            return carry

        lax.fori_loop(0, 4, step, 0)

    def block(mat, xd, h):
        first = pl.multiple_of((div(xd, 2) + 2 * h) * 128, 128)
        return part.at[mat, rem(xd, 2), pl.ds(first, 128), :]

    def x_move(mat, kind, xd, h, way):
        send(
            block(mat, xd, h), xbuf.at[way, mat, kind], x_send,
            x_recv.at[way, mat, kind], device(z, y, xr if way == 0 else xl, s),
        )

    def x_wait(way, mat, kind):
        drain(xbuf.at[way, mat, kind], x_recv.at[way, mat, kind])

    def x_first(mat):
        x_move(mat, 0, x2, 0, 0)
        x_move(mat, 0, x2, 1, 1)
        x_move(mat, 1, xr, 1, 0)
        x_move(mat, 1, xl, 0, 1)

    def x_second(mat):
        for way, xd in ((0, xr), (1, xl)):
            x_wait(way, mat, 0)
            mine = block(mat, xd, way)
            mine[...] = mine[...] + xbuf[way, mat, 0]
            x_move(mat, 2, xd, way, way)

    def x_last(mat):
        for way in range(2):
            for kind in (1, 2):
                x_wait(way, mat, kind)
        for h in range(2):
            mine = block(mat, x, h)
            for c in range(4):
                at = slice(c * 128, (c + 1) * 128)
                red[mat, h * 4 + c] = mine[:, at] + (
                    xbuf[0, mat, 2 - h, :, at] + xbuf[1, mat, 1 + h, :, at]
                )

        def step(n, carry):
            zz = rem(z + n, 8)
            send(
                red.at[mat, zz], zbuf.at[mat, 7 - n], z_send, z_recv.at[mat],
                device(zz, y, x, s),
            )
            return carry

        lax.fori_loop(1, 8, step, 0)

    def z_last(mat, out_ref):
        drain(zbuf.at[mat], z_recv.at[mat])
        total = red[mat, z]
        for n in range(7):
            total = total + zbuf[mat, n]
        out_ref[...] = total

    lax.fori_loop(0, 16, set_left, 0)
    mine_at = jnp.where(role_a, own, 2)
    set_right(lambda at: orb[mine_at, at, :])
    multiply(0)
    x_first(0)

    @pl.when(role_b)
    def _():
        def hand_over(t, carry):
            g, first = rows_of(t)
            arrived(t, g)
            piece = app.at[pl.ds(first, 64)]
            send(piece, piece, d_send, d_recv, sibling)
            return carry

        lax.fori_loop(0, 8, hand_over, 0)

    @pl.when(role_a)
    def _():
        drain(app, d_recv)

    set_right(lambda at: app[at, :])
    multiply(1)
    x_second(0)
    x_first(1)
    x_last(0)
    x_second(1)
    x_last(1)
    z_last(0, ovl_ref)
    z_last(1, ham_ref)

    drain(orb.at[0, pl.ds(0, 504)], a_send)

    @pl.when(role_a)
    def _():
        drain(orb.at[pl.ds(0, 2)], y_send)

    @pl.when(role_b)
    def _():
        drain(orb.at[0], y_send)

    drain(app, d_send)
    drain(xbuf, x_send)
    drain(zbuf, z_send)


def shards(orbitals, applied):
    f32, dma = jnp.float32, pltpu.SemaphoreType.DMA
    tile = jax.ShapeDtypeStruct((128, 128), f32)
    ham, ovl = pl.pallas_call(
        kernel,
        out_shape=(tile, tile),
        in_specs=[pl.BlockSpec(memory_space=pl.ANY)] * 2,
        out_specs=(pl.BlockSpec(memory_space=pltpu.VMEM),) * 2,
        scratch_shapes=[
            pltpu.VMEM((2, 8, 28672), f32),
            pltpu.VMEM((3, 512, DEPTH), f32),
            pltpu.VMEM((512, DEPTH), f32),
            pltpu.VMEM((2, 512, 3 * DEPTH), jnp.bfloat16),
            pltpu.VMEM((512, 3 * DEPTH), jnp.bfloat16),
            pltpu.VMEM((2, 2, 512, 512), f32),
            pltpu.VMEM((2, 2, 3, 128, 512), f32),
            pltpu.VMEM((2, 8, 128, 128), f32),
            pltpu.VMEM((2, 7, 128, 128), f32),
            dma((2,)), dma, dma, dma((8,)), dma, dma((2, 8)), dma, dma,
            dma, dma((2, 2, 3)), dma, dma((2,)),
        ],
        compiler_params=pltpu.CompilerParams(
            collective_id=0, has_side_effects=True, vmem_limit_bytes=56 * 1024 * 1024
        ),
    )(orbitals, applied)
    return ham, ovl


def solution(mesh):
    placed = (P(("row", "col"), None),) * 2
    out = P("col", "row")
    return jax.shard_map(
        shards, mesh=mesh, in_specs=placed, out_specs=(out, out), check_vma=False
    )
```

time: 516 us -> 108 us (0.21)
  the two profiles are of different devices: /device:TPU:6 before, /device:TPU:10 now
where the time goes in v2:
time: 108 us
  Pallas kernels  105 us (97%)
  local copies, waits for them, and re-layouts  2.14 us (2%)
    pallas_call x1, Pallas kernels, shards(): pl.pallas_call(kernel, out_shape=(tile, tile), in_specs=[pl.BlockSpec(mem...  105 us

profile of v2, /device:TPU:10, one launch (start us, length us, event | category | flops | bytes accessed | tf_op | source)
XLA Modules:
  0.0 108.2 jit_solution(1191781794652472157)
XLA Ops:
  0.6 105.4 %shard_map.41 = (f32[128,128]{1,0:T(8,128)}, f32[128,128]{1,0:T(8,128)}) custom-call(f32[8,28672]{1,0:T(8,128)} %orb_hbm.1, f32[8,28672]{1,0:T(8,128)} %app_hbm.1), custom_call_target="tpu_custom_call" | custom-call | tf_op jit(solution)/shard_map/pallas_call | solution.py:302
  106.0 0.0 copy-start
  106.1 1.5 %copy.6 = f32[128,128]{1,0:T(8,128)} copy(f32[128,128]{1,0:T(8,128)} %get-tuple-element.4) | data formatting | bytes 131072
  107.6 0.0 copy-done
  107.6 0.6 copy.7
Async XLA Ops:
  106.0 1.5 %copy-start = (f32[128,128]{1,0:T(8,128)S(1)}, f32[128,128]{1,0:T(8,128)}, u32[]{:S(2)}) copy-start(f32[128,128]{1,0:T(8,128)} %get-tuple-element.5) | copy-start | bytes 196612

commit v3 on v2

v3 whole, which is shorter than its diff:
```python
import jax
import jax.numpy as jnp
from jax import lax
from jax.experimental import pallas as pl
from jax.experimental.pallas import tpu as pltpu
from jax.sharding import PartitionSpec as P

MESH = pl.DeviceIdType.MESH
DEPTH = 896
div, rem = lax.div, lax.rem


def drain(ref, sem):
    pltpu.make_async_copy(ref, ref, sem).wait()


def offset_at(t):
    odd = rem(t, 2)
    return odd * div(t + 1, 2) + (1 - odd) * rem(8 - div(t, 2), 8)


def split3(value, low_at):
    hi = value.astype(jnp.bfloat16)
    lo = (value - hi.astype(jnp.float32)).astype(jnp.bfloat16)
    return [lo if n == low_at else hi for n in range(3)]


def kernel(
    orb_hbm, app_hbm, ham_ref, ovl_ref,
    inp, orb, app, left, right, part, xbuf, red, zbuf,
    in_sem, loc_sem, a_send, a_recv, y_send, y_recv, d_send, d_recv,
    x_send, x_recv, z_send, z_recv,
):
    row, col = lax.axis_index("row"), lax.axis_index("col")
    zl, y = div(row, 4), rem(row, 4)
    zh, x, s = div(col, 8), rem(div(col, 2), 4), rem(col, 2)
    z = zh * 4 + zl
    giver = rem(y, 2)
    role_a = s == giver
    role_b = s != giver
    own = div(y, 2)

    def device(zz, yy, xx, ss):
        return (rem(zz, 4) * 4 + yy, div(zz, 4) * 8 + xx * 2 + ss)

    def send(src, dst, send_sem, recv_sem, target):
        pltpu.make_async_remote_copy(
            src_ref=src, dst_ref=dst, send_sem=send_sem, recv_sem=recv_sem,
            device_id=target, device_id_type=MESH,
        ).start()

    sibling = device(z, y, x, 1 - s)
    y_up, y_down = device(z, rem(y + 1, 4), x, s), device(z, rem(y + 3, 4), x, s)
    xr, xl = rem(x + 1, 4), rem(x + 3, 4)

    loads = [
        pltpu.make_async_copy(orb_hbm, inp.at[0], in_sem.at[0]),
        pltpu.make_async_copy(app_hbm, inp.at[1], in_sem.at[1]),
    ]
    for load in loads:
        load.start()

    barrier = pltpu.get_barrier_semaphore()

    def greet(n, carry):
        p = rem(z * 8 + x * 2 + s + n, 64)
        pl.semaphore_signal(
            barrier, inc=1, device_id=device(div(p, 8), y, div(rem(p, 8), 2), rem(p, 2)),
            device_id_type=MESH,
        )
        return carry

    lax.fori_loop(1, 64, greet, 0)
    for target in (y_up, y_down):
        pl.semaphore_signal(barrier, inc=1, device_id=target, device_id_type=MESH)
    for load in loads:
        load.wait()
    pl.semaphore_wait(barrier, 65)

    slot = pl.ds(pl.multiple_of(zl * 128 + col * 8, 8), 8)
    orb_slot, app_slot = orb.at[own, slot], app.at[slot]

    def columns(zz, xx):
        return pl.ds(pl.multiple_of((zz * 4 + xx) * DEPTH, 128), DEPTH)

    def scatter(which, dst, core):
        def step(n, carry):
            d = offset_at(div(n, 4))
            zz, xx = rem(z + d, 8), rem(x + rem(n, 4), 4)
            send(
                inp.at[which, :, columns(zz, xx)], dst, a_send,
                a_recv.at[rem(8 - d, 8)], device(zz, y, xx, core),
            )
            return carry

        lax.fori_loop(1, 32, step, 0)

    orb_mine, app_mine = inp.at[0, :, columns(z, x)], inp.at[1, :, columns(z, x)]

    @pl.when(role_a)
    def _():
        pltpu.make_async_copy(orb_mine, orb_slot, loc_sem).start()

    @pl.when(role_b)
    def _():
        send(orb_mine, orb_slot, a_send, a_recv.at[0], sibling)

    scatter(0, orb_slot, giver)

    @pl.when(role_a)
    def _():
        send(app_mine, app_slot, a_send, a_recv.at[0], sibling)

    @pl.when(role_b)
    def _():
        pltpu.make_async_copy(app_mine, app_slot, loc_sem).start()

    scatter(1, app_slot, 1 - giver)

    def rows_of(t):
        g = offset_at(t)
        zz = rem(z + g, 8)
        return g, pl.multiple_of(rem(zz, 4) * 128 + div(zz, 4) * 64, 64)

    def arrived(t, g):
        @pl.when(t == 0)
        def _():
            drain(app.at[pl.ds(0, 56)], a_recv.at[0])
            drain(app.at[pl.ds(0, 8)], loc_sem)

        @pl.when(t > 0)
        def _():
            drain(app.at[pl.ds(0, 64)], a_recv.at[g])

    def neighbour(way):
        return device(z, y, xr if way == 0 else xl, s)

    below, above = div(rem(y + 3, 4), 2), div(rem(y + 1, 4), 2)

    def pass_own(t, carry):
        g, first = rows_of(t)
        arrived(t, g)
        block = orb.at[own, pl.ds(first, 64)]
        send(block, block, y_send, y_recv.at[0, g], y_up)
        send(block, block, y_send, y_recv.at[1, g], y_down)
        send(block, orb.at[2, pl.ds(first, 64)], d_send, d_recv, sibling)
        return carry

    def pass_others(t):
        g, first = rows_of(t)
        drain(app.at[pl.ds(0, 64)], y_recv.at[0, g])
        low = orb.at[below, pl.ds(first, 32)]
        send(low, low, y_send, y_recv.at[0, g], y_up)
        drain(app.at[pl.ds(0, 64)], y_recv.at[1, g])
        high = orb.at[above, pl.ds(first + 32, 32)]
        send(high, high, y_send, y_recv.at[1, g], y_down)

    def take(t):
        g, _ = rows_of(t)
        for way in range(2):
            drain(app.at[pl.ds(0, 32)], y_recv.at[way, g])

    def hand_over(t):
        g, first = rows_of(t)
        arrived(t, g)
        piece = app.at[pl.ds(first, 64)]
        send(piece, piece, d_send, d_recv, sibling)

    def set_left(t):
        _, first = rows_of(t)
        for q in range(2):
            to = pl.ds(pl.multiple_of((t * 2 + q) * 64, 64), 64)
            for k, piece in enumerate(split3(orb[q, pl.ds(first, 64), :], 1)):
                left[to, k * DEPTH : (k + 1) * DEPTH] = piece

    def set_right(read):
        def step(n, carry):
            at = pl.ds(pl.multiple_of(n * 64, 64), 64)
            for k, piece in enumerate(split3(read(at), 2)):
                right[at, k * DEPTH : (k + 1) * DEPTH] = piece
            return carry

        lax.fori_loop(0, 8, step, 0)

    def multiply(mat, p):
        got = lax.dot_general(
            left[pl.ds(pl.multiple_of(p * 256, 256), 256), :], right[...],
            (((1,), (1,)), ((), ())), preferred_element_type=jnp.float32,
        )
        part[pl.ds(mat * 16 + p * 4, 4)] = got.reshape(4, 64, 512)

    def place(t, q):
        zz = rem(z + offset_at(t), 8)
        zl_t = rem(zz, 4)
        return rem(2 * rem(zl_t, 2) + q + 4 - x, 4), div(zl_t, 2), div(zz, 4)

    def x_move(n, way):
        send(
            part.at[n], xbuf.at[way, n], x_send, x_recv.at[way, n], neighbour(way)
        )

    def x_wait(n, way):
        drain(xbuf.at[way, n], x_recv.at[way, n])

    def x_first(mat, t):
        for q in range(2):
            n = mat * 16 + t * 2 + q
            far, h, _ = place(t, q)
            for way, near in ((0, 1), (1, 3)):

                @pl.when(((far == 2) & (h == way)) | ((far == near) & (h == 1 - way)))
                def _(n=n, way=way):
                    x_move(n, way)

    def x_second(mat, t):
        for q in range(2):
            n = mat * 16 + t * 2 + q
            far, h, _ = place(t, q)
            for way, near in ((0, 1), (1, 3)):

                @pl.when((far == near) & (h == way))
                def _(n=n, way=way):
                    x_wait(n, way)
                    part[n] = part[n] + xbuf[way, n]
                    x_move(n, way)

    def x_last(mat, t):
        for q in range(2):
            n = mat * 16 + t * 2 + q
            far, h, r = place(t, q)

            @pl.when(far == 0)
            def _(n=n, h=h, r=r):
                x_wait(n, 0)
                x_wait(n, 1)
                half = pl.ds(pl.multiple_of(r * 64, 64), 64)
                for c in range(4):
                    at = slice(c * 128, (c + 1) * 128)
                    zz = h * 4 + c
                    red[mat, zz, half] = part[n, :, at] + (
                        xbuf[0, n, :, at] + xbuf[1, n, :, at]
                    )

                    @pl.when(zz != z)
                    def _(zz=zz):
                        send(
                            red.at[mat, zz, half],
                            zbuf.at[mat, rem(z - zz + 8, 8) - 1, half],
                            z_send, z_recv.at[mat], device(zz, y, x, s),
                        )

    def z_last(mat, out_ref):
        drain(zbuf.at[mat], z_recv.at[mat])
        total = red[mat, z]
        for n in range(7):
            total = total + zbuf[mat, n]
        out_ref[...] = total

    def pair(p, action):
        action(2 * p)
        action(2 * p + 1)

    @pl.when(role_a)
    def _():
        lax.fori_loop(0, 8, pass_own, 0)

    @pl.when(role_b)
    def _():
        def step(t, carry):
            pass_others(t)
            return carry

        lax.fori_loop(0, 4, step, 0)
        drain(app, d_recv)

    mine_at = jnp.where(role_a, own, 2)
    set_right(lambda at: orb[mine_at, at, :])

    def overlaps(p, carry):
        @pl.when(role_a)
        def _():
            pair(p, take)

        @pl.when(role_b & (p >= 2))
        def _():
            pair(p, pass_others)

        pair(p, set_left)
        multiply(0, p)
        pair(p, lambda t: x_first(0, t))

        @pl.when(p >= 2)
        def _():
            pair(p - 2, lambda t: x_second(0, t))

        @pl.when(role_b & (p >= 1))
        def _():
            pair(p - 1, hand_over)

        return carry

    lax.fori_loop(0, 4, overlaps, 0)

    @pl.when(role_b)
    def _():
        pair(3, hand_over)

    @pl.when(role_a)
    def _():
        drain(app, d_recv)

    set_right(lambda at: app[at, :])

    def energies(p, carry):
        multiply(1, p)
        pair(p, lambda t: x_first(1, t))

        @pl.when(p < 2)
        def _():
            pair(p + 2, lambda t: x_second(0, t))

        return carry

    lax.fori_loop(0, 4, energies, 0)

    def finish(p, carry):
        pair(p, lambda t: x_last(0, t))
        pair(p, lambda t: x_second(1, t))
        return carry

    lax.fori_loop(0, 4, finish, 0)

    def close(p, carry):
        pair(p, lambda t: x_last(1, t))
        return carry

    lax.fori_loop(0, 4, close, 0)
    z_last(0, ovl_ref)
    z_last(1, ham_ref)

    drain(orb.at[0, pl.ds(0, 504)], a_send)

    @pl.when(role_a)
    def _():
        drain(orb.at[pl.ds(0, 2)], y_send)

    @pl.when(role_b)
    def _():
        drain(orb.at[0], y_send)

    drain(app, d_send)
    drain(xbuf.at[0, pl.ds(0, 24)], x_send)
    drain(zbuf, z_send)


def shards(orbitals, applied):
    f32, dma = jnp.float32, pltpu.SemaphoreType.DMA
    tile = jax.ShapeDtypeStruct((128, 128), f32)
    ham, ovl = pl.pallas_call(
        kernel,
        out_shape=(tile, tile),
        in_specs=[pl.BlockSpec(memory_space=pl.ANY)] * 2,
        out_specs=(pl.BlockSpec(memory_space=pltpu.VMEM),) * 2,
        scratch_shapes=[
            pltpu.VMEM((2, 8, 28672), f32),
            pltpu.VMEM((3, 512, DEPTH), f32),
            pltpu.VMEM((512, DEPTH), f32),
            pltpu.VMEM((1024, 3 * DEPTH), jnp.bfloat16),
            pltpu.VMEM((512, 3 * DEPTH), jnp.bfloat16),
            pltpu.VMEM((32, 64, 512), f32),
            pltpu.VMEM((2, 32, 64, 512), f32),
            pltpu.VMEM((2, 8, 128, 128), f32),
            pltpu.VMEM((2, 7, 128, 128), f32),
            dma((2,)), dma, dma, dma((8,)), dma, dma((2, 8)), dma, dma,
            dma, dma((2, 32)), dma, dma((2,)),
        ],
        compiler_params=pltpu.CompilerParams(
            collective_id=0, has_side_effects=True, vmem_limit_bytes=56 * 1024 * 1024
        ),
    )(orbitals, applied)
    return ham, ovl


def solution(mesh):
    placed = (P(("row", "col"), None),) * 2
    out = P("col", "row")
    return jax.shard_map(
        shards, mesh=mesh, in_specs=placed, out_specs=(out, out), check_vma=False
    )
```

time: 108 us -> 94 us (0.87)
  the two profiles are of different devices: /device:TPU:10 before, /device:TPU:6 now
where the time goes in v3:
time: 94 us; the launch traced here: 93.8 us
  Pallas kernels  91 us (97%)
  local copies, waits for them, and re-layouts  2.14 us (2%)
    pallas_call x1, Pallas kernels, shards(): pl.pallas_call(kernel, out_shape=(tile, tile), in_specs=[pl.BlockSpec(mem...  91 us
    unnamed x4, local copies, waits for them, and re-layouts  2.14 us

profile of v3, /device:TPU:6, one launch (start us, length us, event | category | flops | bytes accessed | tf_op | source)
XLA Modules:
  0.0 93.8 jit_solution(7116683559921689773)
XLA Ops:
  0.6 91.0 %shard_map.41 = (f32[128,128]{1,0:T(8,128)}, f32[128,128]{1,0:T(8,128)}) custom-call(f32[8,28672]{1,0:T(8,128)} %orb_hbm.1, f32[8,28672]{1,0:T(8,128)} %app_hbm.1), custom_call_target="tpu_custom_call" | custom-call | tf_op jit(solution)/shard_map/pallas_call | solution.py:359
  91.7 0.0 copy-start
  91.7 1.5 %copy.6 = f32[128,128]{1,0:T(8,128)} copy(f32[128,128]{1,0:T(8,128)} %get-tuple-element.4) | data formatting | bytes 131072
  93.2 0.0 copy-done
  93.2 0.6 copy.7
Async XLA Ops:
  91.7 1.5 %copy-start = (f32[128,128]{1,0:T(8,128)S(1)}, f32[128,128]{1,0:T(8,128)}, u32[]{:S(2)}) copy-start(f32[128,128]{1,0:T(8,128)} %get-tuple-element.5) | copy-start | bytes 196612

commit v4 on v3

--- a/solution.py
+++ b/solution.py
@@ -7,6 +7,7 @@
 
 MESH = pl.DeviceIdType.MESH
 DEPTH = 896
+EAGER = 4
 div, rem = lax.div, lax.rem
 
 
@@ -27,9 +28,9 @@
 
 def kernel(
     orb_hbm, app_hbm, ham_ref, ovl_ref,
-    inp, orb, app, left, right, part, xbuf, red, zbuf,
+    inp, orb, app, left, right, part, xbuf, red, zbuf, turned,
     in_sem, loc_sem, a_send, a_recv, y_send, y_recv, d_send, d_recv,
-    x_send, x_recv, z_send, z_recv,
+    x_send, x_recv, z_send, z_recv, t_send, t_recv,
 ):
     row, col = lax.axis_index("row"), lax.axis_index("col")
     zl, y = div(row, 4), rem(row, 4)
@@ -40,6 +41,17 @@
     role_b = s != giver
     own = div(y, 2)
 
+    def turn_of(plane):
+        return jnp.where((plane == 3) | ((plane == 2) & (y >= 2)), 1, 0)
+
+    def plane_of(q):
+        return rem(s + 2 * q + 4 - y, 4)
+
+    row_plane = plane_of(rem(x, 2))
+    tile_at = rem(zl + 8 - (2 * zh + div(x, 2)) - turn_of(row_plane), 4)
+    summed = (row_plane == 0) | (tile_at < 2)
+    mirror = (col, row)
+
     def device(zz, yy, xx, ss):
         return (rem(zz, 4) * 4 + yy, div(zz, 4) * 8 + xx * 2 + ss)
 
@@ -63,19 +75,29 @@
     barrier = pltpu.get_barrier_semaphore()
 
     def greet(n, carry):
-        p = rem(z * 8 + x * 2 + s + n, 64)
+        zz = rem(z + offset_at(7 - n), 8)
+        for i in range(8):
+            pl.semaphore_signal(
+                barrier, inc=1, device_id=(rem(zz, 4) * 4 + y, div(zz, 4) * 8 + i),
+                device_id_type=MESH,
+            )
+        return carry
+
+    @pl.when(row_plane != 0)
+    def _():
+        pl.semaphore_signal(barrier, inc=1, device_id=mirror, device_id_type=MESH)
+
+    lax.fori_loop(0, 7, greet, 0)
+    for i in range(1, 8):
         pl.semaphore_signal(
-            barrier, inc=1, device_id=device(div(p, 8), y, div(rem(p, 8), 2), rem(p, 2)),
+            barrier, inc=1, device_id=(row, zh * 8 + rem(x * 2 + s + i, 8)),
             device_id_type=MESH,
         )
-        return carry
-
-    lax.fori_loop(1, 64, greet, 0)
     for target in (y_up, y_down):
         pl.semaphore_signal(barrier, inc=1, device_id=target, device_id_type=MESH)
     for load in loads:
         load.wait()
-    pl.semaphore_wait(barrier, 65)
+    pl.semaphore_wait(barrier, jnp.where(row_plane == 0, 65, 66))
 
     slot = pl.ds(pl.multiple_of(zl * 128 + col * 8, 8), 8)
     orb_slot, app_slot = orb.at[own, slot], app.at[slot]
@@ -137,28 +159,39 @@
 
     below, above = div(rem(y + 3, 4), 2), div(rem(y + 1, 4), 2)
 
+    def half_of(first, way, half):
+        return pl.ds(pl.multiple_of(first + 32 * rem(way + half, 2), 32), 32)
+
+    def y_move(t, half):
+        g, first = rows_of(t)
+        for way, target in ((0, y_up), (1, y_down)):
+            block = orb.at[own, half_of(first, way, half)]
+            send(block, block, y_send, y_recv.at[way, g, half], target)
+
     def pass_own(t, carry):
         g, first = rows_of(t)
         arrived(t, g)
+        y_move(t, 0)
+
+        @pl.when(t < EAGER)
+        def _():
+            y_move(t, 1)
+
         block = orb.at[own, pl.ds(first, 64)]
-        send(block, block, y_send, y_recv.at[0, g], y_up)
-        send(block, block, y_send, y_recv.at[1, g], y_down)
         send(block, orb.at[2, pl.ds(first, 64)], d_send, d_recv, sibling)
         return carry
 
+    def y_wait(t, half):
+        g, _ = rows_of(t)
+        for way in range(2):
+            drain(app.at[pl.ds(0, 32)], y_recv.at[way, g, half])
+
     def pass_others(t):
         g, first = rows_of(t)
-        drain(app.at[pl.ds(0, 64)], y_recv.at[0, g])
-        low = orb.at[below, pl.ds(first, 32)]
-        send(low, low, y_send, y_recv.at[0, g], y_up)
-        drain(app.at[pl.ds(0, 64)], y_recv.at[1, g])
-        high = orb.at[above, pl.ds(first + 32, 32)]
-        send(high, high, y_send, y_recv.at[1, g], y_down)
-
-    def take(t):
-        g, _ = rows_of(t)
-        for way in range(2):
-            drain(app.at[pl.ds(0, 32)], y_recv.at[way, g])
+        for way, plane, target in ((0, below, y_up), (1, above, y_down)):
+            drain(app.at[pl.ds(0, 32)], y_recv.at[way, g, 0])
+            block = orb.at[plane, half_of(first, way, 0)]
+            send(block, block, y_send, y_recv.at[way, g, 0], target)
 
     def hand_over(t):
         g, first = rows_of(t)
@@ -187,74 +220,97 @@
             left[pl.ds(pl.multiple_of(p * 256, 256), 256), :], right[...],
             (((1,), (1,)), ((), ())), preferred_element_type=jnp.float32,
         )
-        part[pl.ds(mat * 16 + p * 4, 4)] = got.reshape(4, 64, 512)
+        for n in range(4):
+            t, q = p * 2 + n // 2, n % 2
+            _, zl_t, _ = place(t, q)
+            for c in range(4):
+                e = c if mat else rem(c + 8 - zl_t - turn_of(plane_of(q)), 4)
+                part[mat * 16 + p * 4 + n, e] = got[
+                    n * 64 : (n + 1) * 64, c * 128 : (c + 1) * 128
+                ]
 
     def place(t, q):
         zz = rem(z + offset_at(t), 8)
         zl_t = rem(zz, 4)
-        return rem(2 * rem(zl_t, 2) + q + 4 - x, 4), div(zl_t, 2), div(zz, 4)
-
-    def x_move(n, way):
+        return rem(2 * rem(zl_t, 2) + q + 4 - x, 4), zl_t, div(zz, 4)
+
+    def spans(mat, q):
+        if mat:
+            return ((True, 4),)
+        whole = plane_of(q) == 0
+        return ((whole, 4), (jnp.logical_not(whole), 2))
+
+    def x_move(mat, n, way, count):
+        some = pl.ds(0, count)
         send(
-            part.at[n], xbuf.at[way, n], x_send, x_recv.at[way, n], neighbour(way)
+            part.at[n, some], xbuf.at[way, n, some], x_send.at[mat],
+            x_recv.at[way, n], neighbour(way),
         )
 
-    def x_wait(n, way):
-        drain(xbuf.at[way, n], x_recv.at[way, n])
-
-    def x_first(mat, t):
+    def x_wait(n, way, count):
+        drain(xbuf.at[way, n, pl.ds(0, count)], x_recv.at[way, n])
+
+    def pieces(mat, t, action):
         for q in range(2):
             n = mat * 16 + t * 2 + q
-            far, h, _ = place(t, q)
+            far, zl_t, r = place(t, q)
+            for cond, count in spans(mat, q):
+                action(n, q, far, zl_t, r, cond, count)
+
+    def x_first(mat, t):
+        def action(n, q, far, zl_t, r, cond, count):
+            h = div(zl_t, 2)
             for way, near in ((0, 1), (1, 3)):
 
-                @pl.when(((far == 2) & (h == way)) | ((far == near) & (h == 1 - way)))
-                def _(n=n, way=way):
-                    x_move(n, way)
+                @pl.when(
+                    cond & (((far == 2) & (h == way)) | ((far == near) & (h == 1 - way)))
+                )
+                def _(way=way):
+                    x_move(mat, n, way, count)
+
+        pieces(mat, t, action)
 
     def x_second(mat, t):
-        for q in range(2):
-            n = mat * 16 + t * 2 + q
-            far, h, _ = place(t, q)
+        def action(n, q, far, zl_t, r, cond, count):
             for way, near in ((0, 1), (1, 3)):
 
-                @pl.when((far == near) & (h == way))
-                def _(n=n, way=way):
-                    x_wait(n, way)
-                    part[n] = part[n] + xbuf[way, n]
-                    x_move(n, way)
+                @pl.when(cond & (far == near) & (div(zl_t, 2) == way))
+                def _(way=way):
+                    x_wait(n, way, count)
+                    some = pl.ds(0, count)
+                    part[n, some] = part[n, some] + xbuf[way, n, some]
+                    x_move(mat, n, way, count)
+
+        pieces(mat, t, action)
 
     def x_last(mat, t):
-        for q in range(2):
-            n = mat * 16 + t * 2 + q
-            far, h, r = place(t, q)
-
-            @pl.when(far == 0)
-            def _(n=n, h=h, r=r):
-                x_wait(n, 0)
-                x_wait(n, 1)
+        def action(n, q, far, zl_t, r, cond, count):
+            @pl.when(cond & (far == 0))
+            def _():
+                x_wait(n, 0, count)
+                x_wait(n, 1, count)
                 half = pl.ds(pl.multiple_of(r * 64, 64), 64)
-                for c in range(4):
-                    at = slice(c * 128, (c + 1) * 128)
-                    zz = h * 4 + c
-                    red[mat, zz, half] = part[n, :, at] + (
-                        xbuf[0, n, :, at] + xbuf[1, n, :, at]
-                    )
+                for e in range(count):
+                    c = e if mat else rem(zl_t + turn_of(plane_of(q)) + e, 4)
+                    zz = div(zl_t, 2) * 4 + c
+                    red[mat, zz, half] = part[n, e] + (xbuf[0, n, e] + xbuf[1, n, e])
 
                     @pl.when(zz != z)
                     def _(zz=zz):
                         send(
                             red.at[mat, zz, half],
                             zbuf.at[mat, rem(z - zz + 8, 8) - 1, half],
-                            z_send, z_recv.at[mat], device(zz, y, x, s),
+                            z_send.at[mat], z_recv.at[mat], device(zz, y, x, s),
                         )
 
-    def z_last(mat, out_ref):
+        pieces(mat, t, action)
+
+    def z_sum(mat):
         drain(zbuf.at[mat], z_recv.at[mat])
         total = red[mat, z]
         for n in range(7):
             total = total + zbuf[mat, n]
-        out_ref[...] = total
+        return total
 
     def pair(p, action):
         action(2 * p)
@@ -264,6 +320,12 @@
     def _():
         lax.fori_loop(0, 8, pass_own, 0)
 
+        def rest(t, carry):
+            y_move(t, 1)
+            return carry
+
+        lax.fori_loop(EAGER, 8, rest, 0)
+
     @pl.when(role_b)
     def _():
         def step(t, carry):
@@ -279,19 +341,23 @@
     def overlaps(p, carry):
         @pl.when(role_a)
         def _():
-            pair(p, take)
-
-        @pl.when(role_b & (p >= 2))
-        def _():
-            pair(p, pass_others)
+            pair(p, lambda t: y_wait(t, 0))
+
+        @pl.when(role_b & (p < 2))
+        def _():
+            pair(p + 2, pass_others)
+
+        @pl.when(role_b)
+        def _():
+            pair(p, lambda t: y_wait(t, 1))
 
         pair(p, set_left)
         multiply(0, p)
         pair(p, lambda t: x_first(0, t))
 
-        @pl.when(p >= 2)
-        def _():
-            pair(p - 2, lambda t: x_second(0, t))
+        @pl.when(p >= 1)
+        def _():
+            pair(p - 1, lambda t: x_second(0, t))
 
         @pl.when(role_b & (p >= 1))
         def _():
@@ -313,30 +379,49 @@
 
     def energies(p, carry):
         multiply(1, p)
-        pair(p, lambda t: x_first(1, t))
 
         @pl.when(p < 2)
         def _():
-            pair(p + 2, lambda t: x_second(0, t))
+            pair(p, lambda t: x_first(1, t))
+
+        @pl.when(p == 0)
+        def _():
+            pair(3, lambda t: x_second(0, t))
 
         return carry
 
     lax.fori_loop(0, 4, energies, 0)
-
-    def finish(p, carry):
-        pair(p, lambda t: x_last(0, t))
-        pair(p, lambda t: x_second(1, t))
-        return carry
-
-    lax.fori_loop(0, 4, finish, 0)
-
-    def close(p, carry):
-        pair(p, lambda t: x_last(1, t))
-        return carry
-
-    lax.fori_loop(0, 4, close, 0)
-    z_last(0, ovl_ref)
-    z_last(1, ham_ref)
+    pair(0, lambda t: x_last(0, t))
+    pair(1, lambda t: x_last(0, t))
+    pair(0, lambda t: x_second(1, t))
+    pair(2, lambda t: x_first(1, t))
+    pair(2, lambda t: x_last(0, t))
+    pair(1, lambda t: x_second(1, t))
+    pair(3, lambda t: x_first(1, t))
+    pair(3, lambda t: x_last(0, t))
+    pair(2, lambda t: x_second(1, t))
+    pair(0, lambda t: x_last(1, t))
+    pair(1, lambda t: x_last(1, t))
+    pair(3, lambda t: x_second(1, t))
+    pair(2, lambda t: x_last(1, t))
+
+    @pl.when(summed)
+    def _():
+        total = z_sum(0)
+        ovl_ref[...] = total
+
+        @pl.when(row_plane != 0)
+        def _():
+            turned[0] = total.T
+            send(turned.at[0], turned.at[1], t_send, t_recv, mirror)
+
+    pair(3, lambda t: x_last(1, t))
+    ham_ref[...] = z_sum(1)
+
+    @pl.when(jnp.logical_not(summed))
+    def _():
+        drain(turned.at[1], t_recv)
+        ovl_ref[...] = turned[1]
 
     drain(orb.at[0, pl.ds(0, 504)], a_send)
 
@@ -349,8 +434,30 @@
         drain(orb.at[0], y_send)
 
     drain(app, d_send)
-    drain(xbuf.at[0, pl.ds(0, 24)], x_send)
-    drain(zbuf, z_send)
+
+    def x_done(cond, mat, whole_pieces):
+        @pl.when(cond)
+        def _():
+            drain(xbuf.at[0, pl.ds(0, whole_pieces)], x_send.at[mat])
+
+    x_done(role_b, 0, 6)
+    x_done(role_a & (rem(x, 2) == own), 0, 8)
+    x_done(role_a & (rem(x, 2) != own), 0, 10)
+    x_done(True, 1, 12)
+
+    def z_done(cond, mat, halves):
+        @pl.when(cond)
+        def _():
+            drain(xbuf.at[0, 0:halves, 0], z_send.at[mat])
+
+    z_done(row_plane == 0, 0, 14)
+    z_done((row_plane != 0) & summed, 0, 6)
+    z_done(jnp.logical_not(summed), 0, 8)
+    z_done(True, 1, 14)
+
+    @pl.when(summed & (row_plane != 0))
+    def _():
+        drain(turned.at[0], t_send)
 
 
 def shards(orbitals, applied):
@@ -367,18 +474,28 @@
             pltpu.VMEM((512, DEPTH), f32),
             pltpu.VMEM((1024, 3 * DEPTH), jnp.bfloat16),
             pltpu.VMEM((512, 3 * DEPTH), jnp.bfloat16),
-            pltpu.VMEM((32, 64, 512), f32),
-            pltpu.VMEM((2, 32, 64, 512), f32),
+            pltpu.VMEM((32, 4, 64, 128), f32),
+            pltpu.VMEM((2, 32, 4, 64, 128), f32),
             pltpu.VMEM((2, 8, 128, 128), f32),
             pltpu.VMEM((2, 7, 128, 128), f32),
-            dma((2,)), dma, dma, dma((8,)), dma, dma((2, 8)), dma, dma,
-            dma, dma((2, 32)), dma, dma((2,)),
+            pltpu.VMEM((2, 128, 128), f32),
+            dma((2,)), dma, dma, dma((8,)), dma, dma((2, 8, 2)), dma, dma,
+            dma((2,)), dma((2, 32)), dma((2,)), dma((2,)), dma, dma,
         ],
         compiler_params=pltpu.CompilerParams(
             collective_id=0, has_side_effects=True, vmem_limit_bytes=56 * 1024 * 1024
         ),
     )(orbitals, applied)
-    return ham, ovl
+    return pl.pallas_call(
+        settle, out_shape=(tile, tile),
+        in_specs=[pl.BlockSpec(memory_space=pltpu.VMEM)] * 2,
+        out_specs=(pl.BlockSpec(memory_space=pltpu.VMEM),) * 2,
+    )(ham, ovl)
+
+
+def settle(ham_ref, ovl_ref, ham_out, ovl_out):
+    ham_out[...] = ham_ref[...]
+    ovl_out[...] = ovl_ref[...]
 
 
 def solution(mesh):

time: 94 us -> 89.8 us (0.955)
  Pallas kernels: 91 us -> 88.2 us
  local copies, waits for them, and re-layouts: 2.14 us -> 0 us
    pallas_call x1, Pallas kernels: 91 us -> 86.7 us  [shards(): pl.pallas_call(kernel, out_shape=(tile, tile), in_specs=[pl.BlockSpec(mem...]
    unnamed x4 -> x0, local copies, waits for them, and re-layouts: 2.14 us -> none
    pallas_call x0 -> x1, Pallas kernels: none -> 1.53 us  [shards(): pl.pallas_call(settle, out_shape=(tile, tile), in_specs=[pl.BlockSpec(mem...]
where the time goes in v4:
time: 89.8 us; the launch traced here: 88.8 us
  Pallas kernels  88.2 us (98%)
    pallas_call x1, Pallas kernels, shards(): pl.pallas_call(kernel, out_shape=(tile, tile), in_specs=[pl.BlockSpec(mem...  86.7 us

profile of v4, /device:TPU:6, one launch (start us, length us, event | category | flops | bytes accessed | tf_op | source)
XLA Modules:
  0.0 88.8 jit_solution(5627938309156558959)
XLA Ops:
  0.6 86.7 %shard_map.41 = (f32[128,128]{1,0:T(8,128)}, f32[128,128]{1,0:T(8,128)}) custom-call(f32[8,28672]{1,0:T(8,128)} %orb_hbm.1, f32[8,28672]{1,0:T(8,128)} %app_hbm.1), custom_call_target="tpu_custom_call" | custom-call | tf_op jit(solution)/shard_map/pallas_call | solution.py:466
  87.3 1.5 %shard_map.42 = (f32[128,128]{1,0:T(8,128)}, f32[128,128]{1,0:T(8,128)}) custom-call(f32[128,128]{1,0:T(8,128)} %get-tuple-element.4.ham_ref, f32[128,128]{1,0:T(8,128)} %get-tuple-element.5.ovl_ref), custom_call_target="tpu_custom_call" | custom-call | tf_op jit(solution)/shard_map/pallas_call | solution.py:489

commit v5 on v4

--- a/solution.py
+++ b/solution.py
@@ -240,15 +240,17 @@
         whole = plane_of(q) == 0
         return ((whole, 4), (jnp.logical_not(whole), 2))
 
-    def x_move(mat, n, way, count):
-        some = pl.ds(0, count)
+    def x_move(mat, n, way, count, half):
+        some = (n, pl.ds(0, count), pl.ds(32 * half, 32))
         send(
-            part.at[n, some], xbuf.at[way, n, some], x_send.at[mat],
+            part.at[some], xbuf.at[(way,) + some], x_send.at[mat],
             x_recv.at[way, n], neighbour(way),
         )
 
-    def x_wait(n, way, count):
-        drain(xbuf.at[way, n, pl.ds(0, count)], x_recv.at[way, n])
+    def x_wait(n, way, count, first, rows):
+        drain(
+            xbuf.at[way, n, pl.ds(0, count), pl.ds(first, rows)], x_recv.at[way, n]
+        )
 
     def pieces(mat, t, action):
         for q in range(2):
@@ -259,14 +261,16 @@
 
     def x_first(mat, t):
         def action(n, q, far, zl_t, r, cond, count):
-            h = div(zl_t, 2)
+            @pl.when(cond & (far == 2))
+            def _():
+                for way in range(2):
+                    x_move(mat, n, way, count, way)
+
             for way, near in ((0, 1), (1, 3)):
 
-                @pl.when(
-                    cond & (((far == 2) & (h == way)) | ((far == near) & (h == 1 - way)))
-                )
+                @pl.when(cond & (far == near))
                 def _(way=way):
-                    x_move(mat, n, way, count)
+                    x_move(mat, n, way, count, 1 - way)
 
         pieces(mat, t, action)
 
@@ -274,12 +278,12 @@
         def action(n, q, far, zl_t, r, cond, count):
             for way, near in ((0, 1), (1, 3)):
 
-                @pl.when(cond & (far == near) & (div(zl_t, 2) == way))
+                @pl.when(cond & (far == near))
                 def _(way=way):
-                    x_wait(n, way, count)
-                    some = pl.ds(0, count)
-                    part[n, some] = part[n, some] + xbuf[way, n, some]
-                    x_move(mat, n, way, count)
+                    x_wait(n, way, count, 32 * way, 32)
+                    some = (n, pl.ds(0, count), pl.ds(32 * way, 32))
+                    part[some] = part[some] + xbuf[(way,) + some]
+                    x_move(mat, n, way, count, way)
 
         pieces(mat, t, action)
 
@@ -287,8 +291,8 @@
         def action(n, q, far, zl_t, r, cond, count):
             @pl.when(cond & (far == 0))
             def _():
-                x_wait(n, 0, count)
-                x_wait(n, 1, count)
+                x_wait(n, 0, count, 0, 64)
+                x_wait(n, 1, count, 0, 64)
                 half = pl.ds(pl.multiple_of(r * 64, 64), 64)
                 for e in range(count):
                     c = e if mat else rem(zl_t + turn_of(plane_of(q)) + e, 4)

time: 89.8 us -> 88 us (0.980)
  Pallas kernels: 88.2 us -> 86.1 us
    pallas_call x1, Pallas kernels: 86.7 us -> 84.6 us  [shards(): pl.pallas_call(kernel, out_shape=(tile, tile), in_specs=[pl.BlockSpec(mem...]
where the time goes in v5:
time: 88 us; the launch traced here: 86.8 us
  Pallas kernels  86.1 us (98%)
    pallas_call x1, Pallas kernels, shards(): pl.pallas_call(kernel, out_shape=(tile, tile), in_specs=[pl.BlockSpec(mem...  84.6 us

profile of v5, /device:TPU:6, one launch (start us, length us, event | category | flops | bytes accessed | tf_op | source)
XLA Modules:
  0.0 86.8 jit_solution(1263819202555669720)
XLA Ops:
  0.6 84.6 %shard_map.41 = (f32[128,128]{1,0:T(8,128)}, f32[128,128]{1,0:T(8,128)}) custom-call(f32[8,28672]{1,0:T(8,128)} %orb_hbm.1, f32[8,28672]{1,0:T(8,128)} %app_hbm.1), custom_call_target="tpu_custom_call" | custom-call | tf_op jit(solution)/shard_map/pallas_call | solution.py:470
  85.2 1.5 %shard_map.42 = (f32[128,128]{1,0:T(8,128)}, f32[128,128]{1,0:T(8,128)}) custom-call(f32[128,128]{1,0:T(8,128)} %get-tuple-element.4.ham_ref, f32[128,128]{1,0:T(8,128)} %get-tuple-element.5.ovl_ref), custom_call_target="tpu_custom_call" | custom-call | tf_op jit(solution)/shard_map/pallas_call | solution.py:493

commit v6 on v5

--- a/solution.py
+++ b/solution.py
@@ -7,7 +7,7 @@
 
 MESH = pl.DeviceIdType.MESH
 DEPTH = 896
-EAGER = 4
+EAGER = 5
 div, rem = lax.div, lax.rem
 
 
@@ -406,8 +406,8 @@
     pair(2, lambda t: x_second(1, t))
     pair(0, lambda t: x_last(1, t))
     pair(1, lambda t: x_last(1, t))
+    pair(2, lambda t: x_last(1, t))
     pair(3, lambda t: x_second(1, t))
-    pair(2, lambda t: x_last(1, t))
 
     @pl.when(summed)
     def _():

time: 88 us -> 87.1 us (0.990)
  Pallas kernels: 86.1 us -> 85 us
    pallas_call x1, Pallas kernels: 84.6 us -> 83.5 us  [shards(): pl.pallas_call(kernel, out_shape=(tile, tile), in_specs=[pl.BlockSpec(mem...]
where the time goes in v6:
time: 87.1 us; the launch traced here: 85.7 us
  Pallas kernels  85 us (98%)
    pallas_call x1, Pallas kernels, shards(): pl.pallas_call(kernel, out_shape=(tile, tile), in_specs=[pl.BlockSpec(mem...  83.5 us

profile of v6, /device:TPU:6, one launch (start us, length us, event | category | flops | bytes accessed | tf_op | source)
XLA Modules:
  0.0 85.7 jit_solution(15468002191964898536)
XLA Ops:
  0.6 83.5 %shard_map.41 = (f32[128,128]{1,0:T(8,128)}, f32[128,128]{1,0:T(8,128)}) custom-call(f32[8,28672]{1,0:T(8,128)} %orb_hbm.1, f32[8,28672]{1,0:T(8,128)} %app_hbm.1), custom_call_target="tpu_custom_call" | custom-call | tf_op jit(solution)/shard_map/pallas_call | solution.py:470
  84.1 1.5 %shard_map.42 = (f32[128,128]{1,0:T(8,128)}, f32[128,128]{1,0:T(8,128)}) custom-call(f32[128,128]{1,0:T(8,128)} %get-tuple-element.4.ham_ref, f32[128,128]{1,0:T(8,128)} %get-tuple-element.5.ovl_ref), custom_call_target="tpu_custom_call" | custom-call | tf_op jit(solution)/shard_map/pallas_call | solution.py:493

commit v7 on v6

--- a/solution.py
+++ b/solution.py
@@ -409,6 +409,8 @@
     pair(2, lambda t: x_last(1, t))
     pair(3, lambda t: x_second(1, t))
 
+    pair(3, lambda t: x_last(1, t))
+
     @pl.when(summed)
     def _():
         total = z_sum(0)
@@ -419,7 +421,6 @@
             turned[0] = total.T
             send(turned.at[0], turned.at[1], t_send, t_recv, mirror)
 
-    pair(3, lambda t: x_last(1, t))
     ham_ref[...] = z_sum(1)
 
     @pl.when(jnp.logical_not(summed))

time: 87.1 us -> 90.7 us (1.041)
  the two profiles are of different devices: /device:TPU:6 before, /device:TPU:7 now
where the time goes in v7:
time: 90.7 us; the launch traced here: 90.5 us
  Pallas kernels  89.9 us (99%)
    pallas_call x1, Pallas kernels, shards(): pl.pallas_call(kernel, out_shape=(tile, tile), in_specs=[pl.BlockSpec(mem...  88.3 us

profile of v7, /device:TPU:7, one launch (start us, length us, event | category | flops | bytes accessed | tf_op | source)
XLA Modules:
  0.0 90.5 jit_solution(1044228214190831207)
XLA Ops:
  0.6 88.3 %shard_map.41 = (f32[128,128]{1,0:T(8,128)}, f32[128,128]{1,0:T(8,128)}) custom-call(f32[8,28672]{1,0:T(8,128)} %orb_hbm.1, f32[8,28672]{1,0:T(8,128)} %app_hbm.1), custom_call_target="tpu_custom_call" | custom-call | tf_op jit(solution)/shard_map/pallas_call | solution.py:471
  89.0 1.5 %shard_map.42 = (f32[128,128]{1,0:T(8,128)}, f32[128,128]{1,0:T(8,128)}) custom-call(f32[128,128]{1,0:T(8,128)} %get-tuple-element.4.ham_ref, f32[128,128]{1,0:T(8,128)} %get-tuple-element.5.ovl_ref), custom_call_target="tpu_custom_call" | custom-call | tf_op jit(solution)/shard_map/pallas_call | solution.py:494
